TPU v7x, 32 devices: a whole 2x2x4 slice. The times are simulated.
32 devices in a mesh: dp: 16 (over z, y, x), tensor: 2 (over core).
Axes of the slice: x: 2, y: 2, z: 4, core: 2. Of those that a mesh axis runs over, the one named last changes fastest.
Arguments:
- residual: bfloat16 [512, 6144], P('dp', 'tensor'), may hold values from -16 to 16
- queries: bfloat16 [512, 6144], P('dp', 'tensor'), may hold values from -4.5 to 4.5
- keys: bfloat16 [512, 128, 1024], P('dp', None, 'tensor'), may hold values from -4.5 to 4.5
- values: bfloat16 [512, 128, 1024], P('dp', None, 'tensor'), may hold values from -6 to 6
- lengths: int32 [512], P('dp'), may hold values from 2 to 128
- norm_gain: bfloat16 [6144], P('tensor'), may hold values from 0.099609375 to 1.8984375
- expert_ids: int32 [512, 2], P('dp'), may hold values from 0 to 7, all different within a row; in each aligned block of 32 rows (0 to 31, 32 to 63, ...) at most 16 rows name the same one
- expert_weights: float32 [512, 2], P('dp'), may hold values from 0.2 to 1
- w_in: bfloat16 [6144, 65536], P('tensor', 'dp'), may hold values from -0.078125 to 0.078125
- w_out: bfloat16 [65536, 6144], P('dp', 'tensor'), may hold values from -0.0625 to 0.0625
Outputs:
- output: bfloat16 [512, 6144], P('dp', 'tensor')
Inputs may be any that keep to these rules, and one draw needn't show every extreme that they name: `expert_ids`: each token names 2 different experts; at most 16 of the tokens of one index of dp name one expert, and in every draw some expert is named by exactly 16 of them.
All inputs are finite; a program needn't handle non-finite values.
Results may differ from a plain program's by a relative error of at most 0.008.
Values may be sent and summed in bfloat16 or wider, within the bound.
A program may use at most 128 MiB of HBM per device.

v0:
```python
import functools

import jax
import jax.numpy as jnp
from jax import lax
from jax.experimental import pallas as pl
from jax.experimental.pallas import tpu as pltpu
from jax.sharding import PartitionSpec as P

D = 6144
HEADS = 48
KV = 8
HEAD = 128
EXPERTS = 8
TOPK = 2
CACHE = 128
SRC_CAP = 16


NORM_EPSILON = 1e-05


MESH = pl.DeviceIdType.MESH


def remote(source, target, send_sem, recv_sem, place):
    return pltpu.make_async_remote_copy(
        src_ref=source,
        dst_ref=target,
        send_sem=send_sem,
        recv_sem=recv_sem,
        device_id={"dp": place},
        device_id_type=MESH,
    )


def greet(places):
    barrier = pltpu.get_barrier_semaphore()
    for place in places:
        pl.semaphore_signal(barrier, inc=1, device_id={"dp": place}, device_id_type=MESH)
    pl.semaphore_wait(barrier, len(places))


def far_first(amount):
    return sorted(range(1, amount), key=lambda lap: (-min(lap, amount - lap), lap))


def dispatch_kernel(owners, packed, counts, received, all_counts, plane_send, plane_recv,
                    pair_send, pair_recv, count_send, count_recv, own_sem):
    experts = packed.shape[0]
    places = experts * owners
    me = lax.axis_index("dp")
    expert, owner = lax.div(me, owners), lax.rem(me, owners)
    greet([lax.rem(me + lap, places) for lap in range(1, places)])
    waiting = []
    for lap in range(1, places):
        copy = remote(counts, all_counts.at[me], count_send.at[lap], count_recv.at[lap],
                      lax.rem(me + lap, places))
        copy.start()
        waiting.append(copy)
    own = pltpu.make_async_copy(packed.at[expert], received.at[me], own_sem)
    own.start()
    own_count = pltpu.make_async_copy(counts, all_counts.at[me], count_recv.at[0])
    own_count.start()

    def forward(source, place, lap):
        for step in range(1, owners):
            other = lax.rem(owner + step, owners)
            spot = lap * owners + step
            copy = remote(source, received.at[place], pair_send.at[spot], pair_recv.at[spot],
                          expert * owners + other)
            copy.start()
            waiting.append(copy)

    forward(packed.at[expert], me, 0)
    middle = far_first(experts)
    order = [lap for lap in middle if lap in (1, experts - 1)]
    order += [lap for lap in middle if lap not in (1, experts - 1)]
    for lap in order:
        target = lax.rem(expert + lap, experts)
        copy = remote(packed.at[target], received.at[me], plane_send.at[lap], plane_recv.at[lap],
                      target * owners + owner)
        copy.start()
        waiting.append(copy)
    for lap in order:
        source = lax.rem(expert + experts - lap, experts) * owners + owner
        remote(received.at[source], received.at[source], plane_send.at[lap], plane_recv.at[lap],
               source).wait_recv()
        forward(received.at[source], source, lap)
    for lap in [0] + order:
        for step in range(1, owners):
            other = lax.rem(owner + owners - step, owners)
            place = lax.rem(expert + experts - lap, experts) * owners + other
            spot = lap * owners + step
            remote(received.at[place], received.at[place], pair_send.at[spot], pair_recv.at[spot],
                   expert * owners + other).wait_recv()
    for lap in range(1, places):
        source = lax.rem(me + places - lap, places)
        remote(counts, all_counts.at[source], count_send.at[lap], count_recv.at[lap],
               source).wait_recv()
    own.wait()
    own_count.wait()
    for copy in waiting:
        copy.wait_send()


def dispatch(packed, counts, owners):
    experts, rows, width = packed.shape
    places = experts * owners
    dma = pltpu.SemaphoreType.DMA
    vmem = pl.BlockSpec(memory_space=pltpu.VMEM)
    return pl.pallas_call(
        functools.partial(dispatch_kernel, owners),
        out_shape=(
            jax.ShapeDtypeStruct((places, rows, width), packed.dtype),
            jax.ShapeDtypeStruct((places,) + counts.shape, counts.dtype),
        ),
        in_specs=[vmem, vmem],
        out_specs=(vmem, vmem),
        scratch_shapes=[
            dma((experts,)),
            dma((experts,)),
            dma((places,)),
            dma((places,)),
            dma((places,)),
            dma((places,)),
            dma,
        ],
        compiler_params=pltpu.CompilerParams(collective_id=0, has_side_effects=True),
    )(packed, counts)


def return_kernel(owners, part, out, landed, total, pair_send, pair_recv, plane_send, plane_recv):
    experts = out.shape[0]
    me = lax.axis_index("dp")
    expert, owner = lax.div(me, owners), lax.rem(me, owners)
    greet(
        [lax.rem(expert + lap, experts) * owners + owner for lap in range(1, experts)]
        + [expert * owners + lax.rem(owner + step, owners) for step in range(1, owners)]
    )
    order = far_first(experts) + [0]
    waiting = []
    for lap in order:
        for step in range(1, owners):
            other = lax.rem(owner + step, owners)
            source = lax.rem(expert + lap, experts) * owners + other
            spot = lap * owners + step
            copy = remote(part.at[source], landed.at[spot], pair_send.at[spot], pair_recv.at[spot],
                          expert * owners + other)
            copy.start()
            waiting.append(copy)
    for lap in order:
        target = lax.rem(expert + lap, experts) * owners + owner
        value = part[target].astype(jnp.float32)
        for step in range(1, owners):
            other = lax.rem(owner + owners - step, owners)
            spot = lap * owners + step
            remote(landed.at[spot], landed.at[spot], pair_send.at[spot], pair_recv.at[spot],
                   expert * owners + other).wait_recv()
            value += landed[spot].astype(jnp.float32)
        if lap == 0:
            out[expert] = value.astype(out.dtype)
        else:
            total[lap] = value.astype(total.dtype)
            copy = remote(total.at[lap], out.at[expert], plane_send.at[lap], plane_recv.at[lap],
                          target)
            copy.start()
            waiting.append(copy)
    for lap in order[:-1]:
        source = lax.rem(expert + experts - lap, experts)
        remote(total.at[lap], out.at[source], plane_send.at[lap], plane_recv.at[lap],
               source * owners + owner).wait_recv()
    for copy in waiting:
        copy.wait_send()


def send_back(part, owners):
    places, rows, width = part.shape
    experts = places // owners
    dma = pltpu.SemaphoreType.DMA
    vmem = pl.BlockSpec(memory_space=pltpu.VMEM)
    return pl.pallas_call(
        functools.partial(return_kernel, owners),
        out_shape=jax.ShapeDtypeStruct((experts, rows, width), part.dtype),
        in_specs=[vmem],
        out_specs=vmem,
        scratch_shapes=[
            pltpu.VMEM((places, rows, width), part.dtype),
            pltpu.VMEM((experts, rows, width), part.dtype),
            dma((places,)),
            dma((places,)),
            dma((experts,)),
            dma((experts,)),
        ],
        compiler_params=pltpu.CompilerParams(collective_id=1, has_side_effects=True),
    )(part)


def hidden_kernel(members, chunk, part, out, landed, send_sem, recv_sem):
    me = lax.axis_index("tensor")
    barrier = pltpu.get_barrier_semaphore()
    for step in range(1, members):
        pl.semaphore_signal(
            barrier,
            inc=1,
            device_id={"tensor": lax.rem(me + step, members)},
            device_id_type=MESH,
        )
    pl.semaphore_wait(barrier, members - 1)

    def piece_copy(piece, step):
        rows = pl.ds(piece * chunk, chunk)
        spot = piece * members + step
        return pltpu.make_async_remote_copy(
            src_ref=part.at[rows],
            dst_ref=landed.at[step, rows],
            send_sem=send_sem.at[spot],
            recv_sem=recv_sem.at[spot],
            device_id={"tensor": lax.rem(me + step, members)},
            device_id_type=MESH,
        )

    copies = [
        [piece_copy(piece, step) for step in range(1, members)]
        for piece in range(part.shape[0] // chunk)
    ]
    for row in copies:
        for copy in row:
            copy.start()
    for piece, row in enumerate(copies):
        rows = pl.ds(piece * chunk, chunk)
        value = part[rows].astype(jnp.float32)
        for step, copy in enumerate(row, 1):
            copy.wait_recv()
            value += landed[step, rows].astype(jnp.float32)
        out[rows] = (value / (1.0 + jnp.exp(-value))).astype(out.dtype)
    for row in copies:
        for copy in row:
            copy.wait_send()


def hidden_rows(part):
    members = lax.axis_size("tensor")
    rows = part.shape[0]
    chunk = 32 if rows % 32 == 0 else rows
    dma = pltpu.SemaphoreType.DMA
    vmem = pl.BlockSpec(memory_space=pltpu.VMEM)
    return pl.pallas_call(
        functools.partial(hidden_kernel, members, chunk),
        out_shape=jax.ShapeDtypeStruct(part.shape, part.dtype),
        in_specs=[vmem],
        out_specs=vmem,
        scratch_shapes=[
            pltpu.VMEM((members,) + part.shape, part.dtype),
            dma((members * (rows // chunk),)),
            dma((members * (rows // chunk),)),
        ],
        compiler_params=pltpu.CompilerParams(collective_id=2, has_side_effects=True),
    )(part)


def expert_rows(tok_rows, w_in, w_out):
    partial_sum = jnp.einsum("rd,df->rf", tok_rows, w_in, preferred_element_type=jnp.float32)
    hidden = hidden_rows(partial_sum.astype(jnp.bfloat16))
    return jnp.einsum("rf,fd->rd", hidden, w_out, preferred_element_type=jnp.float32)


def shards(
    residual, queries, keys, values, lengths, norm_gain, expert_ids, expert_weights, w_in, w_out
):
    tokens = residual.shape[0]
    width_local = residual.shape[1]
    head_groups = keys.shape[2] // HEAD
    group_size = HEADS // KV
    query_rows = queries.reshape(tokens, head_groups, group_size, HEAD)
    key_rows = keys.reshape(tokens, CACHE, head_groups, HEAD)
    value_rows = values.reshape(tokens, CACHE, head_groups, HEAD)
    scores = jnp.einsum(
        "tgjd,tlgd->tgjl", query_rows, key_rows, preferred_element_type=jnp.float32
    ) * HEAD ** (-0.5)
    live_mask = (jnp.arange(CACHE, dtype=jnp.int32)[None, :] < lengths[:, None])[:, None, None, :]
    scores = jnp.where(live_mask, scores, -1e30)
    peak_score = jnp.max(scores, axis=-1, keepdims=True)
    powered = jnp.exp(scores - peak_score)
    attention_probs = (powered / jnp.sum(powered, axis=-1, keepdims=True)).astype(jnp.bfloat16)
    attended = jnp.einsum(
        "tgjl,tlgd->tgjd", attention_probs, value_rows, preferred_element_type=jnp.float32
    )
    summed = residual.astype(jnp.float32) + attended.reshape(tokens, width_local)
    square_sums = lax.psum(jnp.sum(summed * summed, axis=1), "tensor")
    normed = (
        summed
        * lax.rsqrt(square_sums[:, None] / D + NORM_EPSILON)
        * norm_gain.astype(jnp.float32)[None, :]
    ).astype(jnp.bfloat16)
    flat_ids = expert_ids.reshape(-1)
    expert_iota = jnp.arange(EXPERTS, dtype=jnp.int32)
    onehot = (flat_ids[:, None] == expert_iota[None, :]).astype(jnp.int32)
    local_rank = jnp.sum(
        (jnp.cumsum(onehot, axis=0, dtype=jnp.int32) - onehot) * onehot, axis=1, dtype=jnp.int32
    )
    counts = jnp.sum(onehot, axis=0, dtype=jnp.int32)
    places = lax.axis_size("dp")
    me = lax.axis_index("dp")
    owners = places // EXPERTS
    capacity = tokens * places * TOPK * 3 // (4 * EXPERTS)
    slot_total = EXPERTS * SRC_CAP
    pair_target = flat_ids * SRC_CAP + local_rank
    pick_pairs = pair_target[None, :] == jnp.arange(slot_total, dtype=jnp.int32)[:, None]
    pick_tokens = jnp.sum(
        pick_pairs.reshape(slot_total, tokens, TOPK).astype(jnp.float32), axis=2
    ).astype(jnp.bfloat16)
    packed = jnp.dot(pick_tokens, normed, preferred_element_type=jnp.float32).astype(jnp.bfloat16)
    padded_counts = jnp.pad(counts[None, :], ((0, 0), (0, 128 - EXPERTS)))
    received, gathered = dispatch(
        packed.reshape(EXPERTS, SRC_CAP, width_local), padded_counts, owners
    )
    all_counts = gathered[:, 0, :EXPERTS]
    place_iota = jnp.arange(places, dtype=jnp.int32)
    offsets = jnp.sum(jnp.where(place_iota[:, None] < me, all_counts, 0), axis=0, dtype=jnp.int32)
    slot_index = local_rank + jnp.sum(onehot * offsets[None, :], axis=1, dtype=jnp.int32)
    keep_mask = slot_index < capacity
    mine = jnp.sum(
        jnp.where(expert_iota[None, :] == me // owners, all_counts, 0), axis=1, dtype=jnp.int32
    )
    before = jnp.sum(
        jnp.where(place_iota[None, :] < place_iota[:, None], mine[None, :], 0),
        axis=1,
        dtype=jnp.int32,
    )
    rank = jnp.arange(SRC_CAP, dtype=jnp.int32)[None, :]
    row_slot = jnp.where(rank < mine[:, None], before[:, None] + rank, -1).reshape(-1)
    pick_rows = (
        row_slot[None, :] == jnp.arange(capacity, dtype=jnp.int32)[:, None]
    ).astype(jnp.bfloat16)
    total_rows = places * SRC_CAP
    compact = jnp.dot(
        pick_rows, received.reshape(total_rows, width_local), preferred_element_type=jnp.float32
    ).astype(jnp.bfloat16)
    results = expert_rows(compact, w_in, w_out).astype(jnp.bfloat16)
    spread = jnp.einsum(
        "cr,cd->rd", pick_rows, results, preferred_element_type=jnp.float32
    ).astype(jnp.bfloat16)
    per_expert = (
        send_back(spread.reshape(places, SRC_CAP, width_local), owners)
        .reshape(slot_total, width_local)
        .astype(jnp.float32)
    )
    pair_weight = expert_weights.reshape(-1) * keep_mask.astype(jnp.float32)
    mix_rows = jnp.sum(
        (pick_pairs.astype(jnp.float32) * pair_weight[None, :]).reshape(slot_total, tokens, TOPK),
        axis=2,
    )
    addition = jnp.einsum("st,sd->td", mix_rows, per_expert, precision=lax.Precision.HIGHEST)
    return (summed + addition).astype(jnp.bfloat16)


def solution(mesh):
    in_specs = (
        P("dp", "tensor"),
        P("dp", "tensor"),
        P("dp", None, "tensor"),
        P("dp", None, "tensor"),
        P("dp"),
        P("tensor"),
        P("dp", None),
        P("dp", None),
        P("tensor", "dp"),
        P("dp", "tensor"),
    )
    out_specs = P("dp", "tensor")
    return jax.shard_map(shards, mesh=mesh, in_specs=in_specs, out_specs=out_specs, check_vma=False)
```

profile of v0, /device:TPU:0, one launch (start us, length us, event | category | flops | bytes accessed | tf_op | source)
XLA Modules:
  0.0 113.9 jit_solution(15608420688407935868)
XLA Ops:
  0.0 0.8 copy.40
  1.0 0.2 fusion.23
  1.2 0.1 reduce_sum.96
  1.4 0.7 multiply_add_fusion
  2.2 1.2 %reshape.139 = bf16[32,4,6,128]{3,2,1,0:T(8,128)(2,1)S(1)} reshape(bf16[32,3072]{1,0:T(8,128)(2,1)} %param.11) | data formatting | bytes 393216 | tf_op jit(solution)/shard_map/reshape | solution.py:275
  3.4 0.7 iota_compare_fusion.6
  4.1 4.6 %fusion.27 = (f32[32,4,6]{2,1,0:T(4,128)S(1)}, f32[32,4,6,128]{3,2,1,0:T(8,128)S(1)}) fusion(bf16[32,4,6,128]{3,2,1,0:T(8,128)(2,1)S(1)} %reshape.139, pred[32,128]{1,0:T(8,128)(4,1)S(1)} %iota_compare_fusion.6, bf16[32,128,512]{2,1,0:T(8,128)(2,1)} %param.12), kind=kOutput, calls=%fused_computation.51 | convolution fusion | flops 25559168 | bytes 4791296 | tf_op jit(solution)/shard_map/sub | solution.py:284
  8.8 3.5 %fusion.1 = f32[32,4,6,128]{3,2,1,0:T(8,128)S(1)} fusion(f32[32,4,6,128]{3,2,1,0:T(8,128)S(1)} %get-tuple-element.14, f32[32,4,6]{2,1,0:T(4,128)S(1)} %get-tuple-element.13, bf16[32,128,512]{2,1,0:T(8,128)(2,1)} %param.13), kind=kOutput, calls=%fused_computation.2 | convolution fusion | flops 25362432 | bytes 4983808 | tf_op jit(solution)/shard_map/tgjl,tlgd->tgjd/dot_general | solution.py:286
  12.3 0.1 reshape.142
  12.4 0.2 multiply_reduce_fusion
  12.5 2.6 %psum.7 = f32[32]{0:T(128)S(1)} all-reduce(f32[32]{0:T(128)S(1)} %multiply_reduce_fusion), channel_id=1, replica_groups=mesh['dp'=16,'tensor'=2] {'tensor'}, use_global_device_ids=true, to_apply=%region_6.7 | all-reduce | flops 32 | bytes 256 | tf_op jit(solution)/shard_map/psum | solution.py:290
  15.2 1.3 %convolution_convert_fusion.2 = bf16[128,3072]{1,0:T(8,128)(2,1)} fusion(f32[3072]{0:T(1024)S(1)} %convert_element_type.48, f32[32]{0:T(128)S(1)} %add_rsqrt_fusion, f32[32,3072]{1,0:T(8,128)S(1)} %reshape.142, bf16[32,3072]{1,0:T(8,128)(2,1)S(1)} %copy-done, bf16[128,32]{0,1:T(8,128)(2,1)S(1)} %convert_reduce_fusion), kind=kOutput, calls=%fused_computation.9 | convolution fusion | flops 26050560 | bytes 1396864 | tf_op jit(solution)/shard_map/dot_general | solution.py:313
  16.5 0.5 pad.4.counts
  17.0 35.4 %shard_map.100 = (bf16[16,16,3072]{2,1,0:T(8,128)(2,1)}, s32[16,1,128]{2,1,0:T(1,128)}) custom-call(bf16[8,16,3072]{2,1,0:T(8,128)(2,1)} %bitcast.44, s32[1,128]{1,0:T(1,128)} %pad.4.counts), custom_call_target="tpu_custom_call" | custom-call | tf_op jit(solution)/shard_map/pallas_call | solution.py:112
  52.4 0.8 copy.42
  53.2 0.1 fusion.26
  53.3 0.1 select_reduce_fusion.3
  53.6 11.9 %convolution_convert_fusion.part = bf16[96,4096]{1,0:T(8,128)(2,1)} fusion(bf16[3072,4096]{1,0:T(8,128)(2,1)} %param.18, bf16[256,3072]{1,0:T(8,128)(2,1)} %bitcast.43, s32[256]{0:T(256)S(1)} %select_n.38), kind=kOutput, calls=%fused_computation.1 | convolution fusion | flops 2567626752 | bytes 27526144 | tf_op jit(solution)/shard_map/rd,df->rf/dot_general | solution.py:263
  65.5 4.6 %shard_map.101 = bf16[96,4096]{1,0:T(8,128)(2,1)} custom-call(bf16[96,4096]{1,0:T(8,128)(2,1)} %convolution_convert_fusion.part), custom_call_target="tpu_custom_call" | custom-call | tf_op jit(solution)/shard_map/pallas_call | solution.py:248
  70.2 14.1 %convolution_convert_fusion.1 = bf16[256,3072]{1,0:T(8,128)(2,1)} fusion(bf16[96,4096]{1,0:T(8,128)(2,1)} %shard_map.101, bf16[4096,3072]{1,0:T(8,128)(2,1)} %param.19, s32[256]{0:T(256)S(1)} %select_n.38), kind=kOutput, calls=%fused_computation.8 | convolution fusion | flops 2568019968 | bytes 27526144 | tf_op jit(solution)/shard_map/cr,cd->rd/dot_general | solution.py:341
  84.2 26.9 %shard_map.102 = bf16[8,16,3072]{2,1,0:T(8,128)(2,1)} custom-call(bf16[16,16,3072]{2,1,0:T(8,128)(2,1)} %bitcast.42), custom_call_target="tpu_custom_call" | custom-call | tf_op jit(solution)/shard_map/pallas_call | solution.py:182
  111.2 0.2 select_reduce_fusion.1
  111.3 0.1 reduce_sum.102
  111.6 2.2 %fusion.7 = bf16[32,3072]{1,0:T(8,128)(2,1)} fusion(f32[128,32]{0,1:T(8,128)S(1)} %select_reduce_fusion, bf16[128,3072]{1,0:T(8,128)(2,1)} %bitcast.45, f32[32,3072]{1,0:T(8,128)S(1)} %reshape.142, bf16[32,3072]{1,0:T(8,128)(2,1)S(1)} %copy-done), kind=kOutput, calls=%fused_computation.13 | convolution fusion | flops 151388160 | bytes 1589248 | tf_op jit(solution)/shard_map/st,sd->td/dot_general | solution.py:354
  (20 shorter events, 0.8 us)
Async XLA Ops:
  8.8 3.6 %copy-start = (bf16[32,3072]{1,0:T(8,128)(2,1)S(1)}, bf16[32,3072]{1,0:T(8,128)(2,1)}, u32[]{:S(2)}) copy-start(bf16[32,3072]{1,0:T(8,128)(2,1)} %param.10) | copy-start | bytes 589828
  8.8 6.4 %copy-start.1 = (bf16[3072]{0:T(1024)(128)(2,1)S(1)}, bf16[3072]{0:T(1024)(128)(2,1)}, u32[]{:S(2)}) copy-start(bf16[3072]{0:T(1024)(128)(2,1)} %param.15) | copy-start | bytes 18436
  70.1 41.4 %copy-start.2 = (f32[32,2]{0,1:T(2,128)S(1)}, f32[32,2]{0,1:T(2,128)}, u32[]{:S(2)}) copy-start(f32[32,2]{0,1:T(2,128)} %param.17) | copy-start | bytes 772
where the time goes:
time: 114 us
  Pallas kernels  66.9 us (59%)
  matrix products  37.7 us (33%)
  local copies, waits for them, and re-layouts  3.9 us (3%)
  other arithmetic  2.64 us (2%)
  blocking collectives  2.62 us (2%)
    pallas_call x1, Pallas kernels, dispatch(): pl.pallas_call(functools.partial(dispatch_kernel, owners), out_shape=(jax...  35.4 us
    pallas_call x1, Pallas kernels, send_back(): pl.pallas_call(functools.partial(return_kernel, owners), out_shape=jax.Sh...  26.9 us
    dot_general x1, matrix products, shards(): jnp.einsum('cr,cd->rd', pick_rows, results, preferred_element_type=jnp.fl...  14.1 us
    dot_general x1, matrix products, expert_rows(): jnp.einsum('rd,df->rf', tok_rows, w_in, preferred_element_type=jnp.float32)  11.9 us
    sub x1, matrix products, shards(): powered = jnp.exp(scores - peak_score)  4.64 us
    pallas_call x1, Pallas kernels, hidden_rows(): pl.pallas_call(functools.partial(hidden_kernel, members, chunk), out_shap...  4.59 us
    dot_general x1, matrix products, shards(): jnp.einsum('tgjl,tlgd->tgjd', attention_probs, value_rows, preferred_elem...  3.47 us
    psum x1, blocking collectives, shards(): square_sums = lax.psum(jnp.sum(summed * summed, axis=1), 'tensor')  2.62 us

commit v1 on v0

--- a/solution.py
+++ b/solution.py
@@ -265,6 +265,466 @@
     return jnp.einsum("rf,fd->rd", hidden, w_out, preferred_element_type=jnp.float32)
 
 
+def slots_of(rows):
+    return -(-rows // 128) * 128
+
+
+def layer_kernel(dims, summed, gain, named, w_in, w_out, out, win, wout, squares, squares_in, gath,
+                 nrm, tok, pick, pick_t, slot_weight, sendx, gotx, acc, part, part_in, hidden,
+                 sendy, goty, weighted, line_out, line_in, fin, extra,
+                 in_sem, out_sem, sq_sem, gath_sem, first_sem, line_sem, third_sem, part_sem,
+                 back_sem, relay_sem, home_sem):
+    lines, planes, owners, chunks, capacity = dims
+    tokens, width = summed.shape
+    members = planes * owners
+    places = lines * members
+    quarter = width // members
+    cols = quarter // chunks
+    group = members * tokens
+    slots = slots_of(capacity)
+    units = w_in.shape[1]
+    me = lax.axis_index("dp")
+    line, spot = lax.div(me, members), lax.rem(me, members)
+    own_plane = lax.div(spot, owners)
+    other_core = 1 - lax.axis_index("tensor")
+    f32, bf16 = jnp.float32, jnp.bfloat16
+
+    def far(source, target, sems, index, device):
+        return pltpu.make_async_remote_copy(
+            src_ref=source, dst_ref=target, send_sem=sems.at[(0,) + index],
+            recv_sem=sems.at[(1,) + index], device_id=device, device_id_type=MESH,
+        )
+
+    def peer(step):
+        return lax.rem(spot + step, members)
+
+    def sender(step):
+        return lax.rem(spot + members - step, members)
+
+    def place(index):
+        return {"dp": line * members + index}
+
+    steps = range(1, members)
+    win_copies = [
+        [
+            pltpu.make_async_copy(
+                w_in.at[pl.ds(q * quarter + c * cols, cols)],
+                win.at[pl.ds((c * members + q) * cols, cols)],
+                in_sem.at[c, q],
+            )
+            for q in range(members)
+        ]
+        for c in range(chunks)
+    ]
+    pieces = out_sem.shape[0]
+    piece = units // pieces
+    wout_copies = [
+        pltpu.make_async_copy(
+            w_out.at[pl.ds(i * piece, piece)], wout.at[pl.ds(i * piece, piece)], out_sem.at[i]
+        )
+        for i in range(pieces)
+    ]
+    barrier = pltpu.get_barrier_semaphore()
+    for lap in range(1, places):
+        pl.semaphore_signal(
+            barrier, inc=1, device_id={"dp": lax.rem(me + lap, places)}, device_id_type=MESH
+        )
+    pl.semaphore_signal(barrier, inc=1, device_id={"tensor": other_core}, device_id_type=MESH)
+    for row in win_copies:
+        for copy in row:
+            copy.start()
+    for copy in wout_copies:
+        copy.start()
+    total = jnp.zeros((tokens, 1), f32)
+    for q in range(members * chunks):
+        value = summed[:, q * cols:(q + 1) * cols]
+        total += jnp.sum(value * value, axis=1, keepdims=True)
+    squares[...] = jnp.broadcast_to(total, squares.shape)
+    pl.semaphore_wait(barrier, places)
+    waiting = []
+    square_copy = far(squares, squares_in, sq_sem, (), {"tensor": other_core})
+    square_copy.start()
+    waiting.append(square_copy)
+    for lap in range(1, places):
+        copy = far(named, gath.at[me], gath_sem, (lap,), {"dp": lax.rem(me + lap, places)})
+        copy.start()
+        waiting.append(copy)
+    gath[me] = named[...]
+    square_copy.wait_recv()
+    scale = lax.rsqrt(
+        (squares[:, :1] + squares_in[:, :1]) / (2 * width) + NORM_EPSILON
+    )
+    for c in range(chunks):
+        for q in range(members):
+            at = q * quarter + c * cols
+            nrm[q, c] = (
+                summed[:, at:at + cols] * scale * gain[:, at:at + cols].astype(f32)
+            ).astype(bf16)
+        home = pl.ds(pl.multiple_of(line * group + spot * tokens, tokens), tokens)
+        tok[c, home] = nrm[spot, c]
+        for step in steps:
+            copy = far(nrm.at[peer(step), c], tok.at[c, home], first_sem, (c, step),
+                       place(peer(step)))
+            copy.start()
+            waiting.append(copy)
+
+    def rows_of(plane):
+        return pl.ds(pl.multiple_of(plane * group, group), group)
+
+    def inside(plane):
+        return (plane >= 0) & (plane < lines)
+
+    def spread(way, c, gap):
+        turn = 1 - 2 * way
+        plane = line - gap * turn
+        rows = rows_of(plane)
+        return inside(plane) & inside(line + turn), far(
+            tok.at[c, rows], tok.at[c, rows], line_sem, (way, c, plane),
+            {"dp": me + turn * members},
+        )
+
+    def arrive(way, c, gap):
+        plane = line - gap * (1 - 2 * way)
+        rows = rows_of(plane)
+        return inside(plane), far(
+            tok.at[c, rows], tok.at[c, rows], line_sem, (way, c, plane), {"dp": me}
+        )
+
+    def begin(pair):
+        @pl.when(pair[0])
+        def _():
+            pair[1].start()
+
+    def landed(pair):
+        @pl.when(pair[0])
+        def _():
+            pair[1].wait_recv()
+
+    def left(pair):
+        @pl.when(pair[0])
+        def _():
+            pair[1].wait_send()
+
+    for c in range(chunks):
+        for step in steps:
+            rows = pl.ds(pl.multiple_of(line * group + sender(step) * tokens, tokens), tokens)
+            far(nrm.at[0, c], tok.at[c, rows], first_sem, (c, step),
+                place(sender(step))).wait_recv()
+        for way in (0, 1):
+            begin(spread(way, c, 0))
+
+    for lap in range(1, places):
+        source = lax.rem(me + places - lap, places)
+        far(named, gath.at[source], gath_sem, (lap,), {"dp": source}).wait_recv()
+    hits, weights = [], []
+    for p in range(lines):
+        tile = gath[p * members]
+        for m in range(1, members):
+            tile += gath[p * members + m]
+        for b in range(planes):
+            expert = (line * planes + b).astype(f32)
+            first, second = tile[0:1] == expert, tile[1:2] == expert
+            hits.append(jnp.where(first | second, 1.0, 0.0))
+            weights.append(jnp.where(first, tile[2:3], jnp.where(second, tile[3:4], 0.0)))
+    earlier = lax.broadcasted_iota(jnp.int32, (group, group), 0)
+    later = lax.broadcasted_iota(jnp.int32, (group, group), 1)
+    before = jnp.where(earlier < later, 1.0, 0.0).astype(bf16)
+    slot_iota = lax.broadcasted_iota(jnp.int32, (slots, group), 0).astype(f32)
+    for b in range(planes):
+        offset = jnp.zeros((1, 1), f32)
+        slot_total = jnp.zeros((slots, 1), f32)
+        for p in range(lines):
+            hit, weight = hits[p * planes + b], weights[p * planes + b]
+            wide = jnp.broadcast_to(hit, (16, group)).astype(bf16)
+            rank = jnp.dot(wide, before, preferred_element_type=f32)[0:1] + offset
+            offset += jnp.sum(hit, axis=1, keepdims=True)
+            rank = jnp.where((hit > 0.0) & (rank < capacity), rank, -1.0)
+            chosen = jnp.where(slot_iota == rank, 1.0, 0.0)
+            pick[b * slots:(b + 1) * slots, p * group:(p + 1) * group] = chosen.astype(bf16)
+            pick_t[p, :, b * slots:(b + 1) * slots] = chosen.T.astype(bf16)
+            slot_total += jnp.sum(chosen * weight, axis=1, keepdims=True)
+        slot_weight[b * slots:(b + 1) * slots] = jnp.broadcast_to(slot_total, (slots, 128))
+    weighted[...] = jnp.zeros_like(weighted)
+
+    def lanes_of(index):
+        return pl.ds(pl.multiple_of(index * cols, 128), cols)
+
+    depth = members * cols
+    block = 512
+    spans = part.shape[0]
+    span = units // spans
+
+    def product(c, at):
+        at = pl.multiple_of(at, 128)
+        return jnp.dot(gotx[c], win[c * depth:(c + 1) * depth, pl.ds(at, block)],
+                       preferred_element_type=f32)
+
+    def expand(c):
+        for step in steps:
+            far(sendx.at[c, 0], gotx.at[c, :, lanes_of(sender(step))], third_sem, (c, step),
+                place(sender(step))).wait_recv()
+        for copy in win_copies[c]:
+            copy.wait()
+        if c < chunks - 1:
+            @pl.loop(0, units // block)
+            def _(i):
+                at = pl.multiple_of(i * block, block)
+                value = product(c, at)
+                acc[:, pl.ds(at, block)] = value if c == 0 else acc[:, pl.ds(at, block)] + value
+            return
+        for h in range(spans):
+            @pl.loop(0, span // block)
+            def _(i):
+                inner = pl.multiple_of(i * block, block)
+                at = h * span + inner
+                value = product(c, at)
+                if c:
+                    value += acc[:, pl.ds(pl.multiple_of(at, block), block)]
+                part[h, :, pl.ds(inner, block)] = value.astype(bf16)
+            copy = far(part.at[h], part_in.at[h], part_sem, (h,), {"tensor": other_core})
+            copy.start()
+            waiting.append(copy)
+
+    for c in range(chunks):
+        for gap in range(1, lines):
+            for way in (0, 1):
+                landed(arrive(way, c, gap))
+                begin(spread(way, c, gap))
+        rows = jnp.dot(pick[...], tok[c], preferred_element_type=f32).astype(bf16)
+        for b in range(planes):
+            sendx[c, b] = rows[b * slots:b * slots + capacity]
+        for step in steps:
+            copy = far(sendx.at[c, lax.div(peer(step), owners)], gotx.at[c, :, lanes_of(spot)],
+                       third_sem, (c, step), place(peer(step)))
+            copy.start()
+            waiting.append(copy)
+        gotx[c, :, lanes_of(spot)] = sendx[c, own_plane]
+        if c:
+            expand(c - 1)
+    expand(chunks - 1)
+    for h in range(spans):
+        far(part.at[h], part_in.at[h], part_sem, (h,), {"tensor": other_core}).wait_recv()
+
+        @pl.loop(0, span // block)
+        def _(i):
+            at = pl.ds(pl.multiple_of(i * block, block), block)
+            value = part[h, :, at].astype(f32) + part_in[h, :, at].astype(f32)
+            value = value / (1.0 + jnp.exp(-value))
+            hidden[:, pl.ds(pl.multiple_of(h * span + i * block, block), block)] = (
+                value.astype(bf16)
+            )
+    for copy in wout_copies:
+        copy.wait()
+
+    def contract(c):
+        for step in list(steps) + [0]:
+            at = pl.multiple_of(peer(step) * quarter + c * cols, 128)
+            value = jnp.dot(hidden[...], wout[:, pl.ds(at, cols)], preferred_element_type=f32)
+            if step:
+                sendy[c, step - 1] = value.astype(bf16)
+                copy = far(sendy.at[c, step - 1], goty.at[c, spot], back_sem, (c, step),
+                           place(peer(step)))
+                copy.start()
+                waiting.append(copy)
+            else:
+                goty[c, spot] = value.astype(bf16)
+
+    def gather_back(c):
+        for step in steps:
+            far(sendy.at[c, 0], goty.at[c, sender(step)], back_sem, (c, step),
+                place(sender(step))).wait_recv()
+        for b in range(planes):
+            value = goty[c, b * owners].astype(f32)
+            for o in range(1, owners):
+                value += goty[c, b * owners + o].astype(f32)
+            value = value * slot_weight[b * slots:b * slots + capacity, :1]
+            weighted[c, b * slots:b * slots + capacity] = value.astype(bf16)
+
+    def share(c, plane):
+        return jnp.dot(pick_t[plane], weighted[c], preferred_element_type=f32)
+
+    def relay_copy(way, c, plane, place_index):
+        return far(line_out.at[way, c, plane], line_in.at[way, c, plane], relay_sem,
+                   (way, c, plane), {"dp": place_index})
+
+    def relay(way, c, gap):
+        turn = 1 - 2 * way
+        plane = line + gap * turn
+
+        @pl.when(inside(plane))
+        def _():
+            value = share(c, plane)
+            line_out[way, c, plane] = value.astype(bf16)
+
+            @pl.when(inside(line - turn))
+            def _():
+                relay_copy(way, c, plane, me - turn * members).wait_recv()
+                line_out[way, c, plane] = (
+                    value + line_in[way, c, plane].astype(f32)
+                ).astype(bf16)
+
+            relay_copy(way, c, plane, me + turn * members).start()
+
+    near = jnp.where(line * 2 < lines, 0, 1)
+
+    def home_copy(c, step):
+        rows = pl.ds(pl.multiple_of(peer(step) * tokens, tokens), tokens)
+        return far(fin.at[c, rows], extra.at[c, spot], home_sem, (c, step), place(peer(step)))
+
+    def finish(c):
+        fin[c] = share(c, line).astype(bf16)
+        for way in (0, 1):
+            turn = 1 - 2 * way
+
+            @pl.when(inside(line - turn))
+            def _():
+                relay_copy(way, c, line, me - turn * members).wait_recv()
+
+        low, high = line > 0, line < lines - 1
+
+        def got(way):
+            return line_in[way, c, line].astype(f32)
+
+        @pl.when(low & high)
+        def _():
+            fin[c] = (share(c, line) + got(0) + got(1)).astype(bf16)
+
+        @pl.when(low & ~high)
+        def _():
+            fin[c] = (share(c, line) + got(0)).astype(bf16)
+
+        @pl.when(high & ~low)
+        def _():
+            fin[c] = (share(c, line) + got(1)).astype(bf16)
+
+        for step in steps:
+            copy = home_copy(c, step)
+            copy.start()
+            waiting.append(copy)
+        extra[c, spot] = fin[c, pl.ds(pl.multiple_of(spot * tokens, tokens), tokens)]
+
+    def close(c):
+        for step in steps:
+            far(fin.at[c, pl.ds(0, tokens)], extra.at[c, sender(step)], home_sem, (c, step),
+                place(sender(step))).wait_recv()
+        for q in range(members):
+            at = q * quarter + c * cols
+            out[:, at:at + cols] = (
+                summed[:, at:at + cols] + extra[c, q].astype(f32)
+            ).astype(out.dtype)
+
+    for c in range(chunks):
+        contract(c)
+        if c:
+            gather_back(c - 1)
+            for gap in range(lines - 1, 1, -1):
+                relay(near, c - 1, gap)
+    gather_back(chunks - 1)
+    for gap in range(lines - 1, 1, -1):
+        relay(near, chunks - 1, gap)
+    for c in range(chunks):
+        relay(near, c, 1)
+    for c in range(chunks):
+        for gap in range(lines - 1, 0, -1):
+            relay(1 - near, c, gap)
+    for c in range(chunks):
+        finish(c)
+        if c:
+            close(c - 1)
+    close(chunks - 1)
+    for copy in waiting:
+        copy.wait_send()
+    for c in range(chunks):
+        for way in (0, 1):
+            for gap in range(lines - 1):
+                left(spread(way, c, gap))
+            turn = 1 - 2 * way
+            for gap in range(1, lines):
+                plane = line + gap * turn
+                left((inside(plane), relay_copy(way, c, plane, me + turn * members)))
+
+
+def layer(summed, gain, named, w_in, w_out, lines, planes, owners, capacity, chunks):
+    tokens, width = summed.shape
+    members = planes * owners
+    cols = width // members // chunks
+    places = lines * members
+    group = members * tokens
+    slots = slots_of(capacity)
+    units = w_in.shape[1]
+    spans, pieces = 4, 8
+    f32, bf16 = jnp.float32, jnp.bfloat16
+    vmem = pl.BlockSpec(memory_space=pltpu.VMEM)
+    hbm = pl.BlockSpec(memory_space=pl.ANY)
+    dma = pltpu.SemaphoreType.DMA
+    return pl.pallas_call(
+        functools.partial(layer_kernel, (lines, planes, owners, chunks, capacity)),
+        out_shape=jax.ShapeDtypeStruct((tokens, width), bf16),
+        in_specs=[vmem, vmem, vmem, hbm, hbm],
+        out_specs=vmem,
+        scratch_shapes=[
+            pltpu.VMEM(w_in.shape, bf16),
+            pltpu.VMEM(w_out.shape, bf16),
+            pltpu.VMEM((tokens, 128), f32),
+            pltpu.VMEM((tokens, 128), f32),
+            pltpu.VMEM((places,) + named.shape, f32),
+            pltpu.VMEM((members, chunks, tokens, cols), bf16),
+            pltpu.VMEM((chunks, lines * group, cols), bf16),
+            pltpu.VMEM((planes * slots, lines * group), bf16),
+            pltpu.VMEM((lines, group, planes * slots), bf16),
+            pltpu.VMEM((planes * slots, 128), f32),
+            pltpu.VMEM((chunks, planes, capacity, cols), bf16),
+            pltpu.VMEM((chunks, capacity, members * cols), bf16),
+            pltpu.VMEM((capacity, units), f32),
+            pltpu.VMEM((spans, capacity, units // spans), bf16),
+            pltpu.VMEM((spans, capacity, units // spans), bf16),
+            pltpu.VMEM((capacity, units), bf16),
+            pltpu.VMEM((chunks, members - 1, capacity, cols), bf16),
+            pltpu.VMEM((chunks, members, capacity, cols), bf16),
+            pltpu.VMEM((chunks, planes * slots, cols), bf16),
+            pltpu.VMEM((2, chunks, lines, group, cols), bf16),
+            pltpu.VMEM((2, chunks, lines, group, cols), bf16),
+            pltpu.VMEM((chunks, group, cols), bf16),
+            pltpu.VMEM((chunks, members, tokens, cols), bf16),
+            dma((chunks, members)),
+            dma((pieces,)),
+            dma((2,)),
+            dma((2, places)),
+            dma((2, chunks, members)),
+            dma((2, 2, chunks, lines)),
+            dma((2, chunks, members)),
+            dma((2, spans)),
+            dma((2, chunks, members)),
+            dma((2, 2, chunks, lines)),
+            dma((2, chunks, members)),
+        ],
+        compiler_params=pltpu.CompilerParams(
+            collective_id=3, has_side_effects=True, vmem_limit_bytes=63 * 1024 * 1024
+        ),
+    )(summed, gain, named, w_in, w_out)
+
+
+def planes_of(places, tokens, width, units, capacity):
+    owners, rest = divmod(places, EXPERTS)
+    planes = 2
+    members = planes * owners
+    if rest or lax.axis_size("tensor") != 2 or members < 2 or members * tokens != 128:
+        return 0
+    if width % (members * 128) or units % 2048 or capacity % 16:
+        return 0
+    held = 4 * units * width + 12 * capacity * units
+    return planes if held < 56 * 1024 * 1024 else 0
+
+
+def named_tile(expert_ids, expert_weights, members):
+    tokens = expert_ids.shape[0]
+    spot = lax.rem(lax.axis_index("dp"), members)
+    rows = jnp.concatenate([expert_ids.astype(jnp.float32), expert_weights], axis=1).T
+    rows = jnp.tile(rows, (1, members))
+    here = jnp.arange(members * tokens, dtype=jnp.int32)[None, :] // tokens == spot
+    return jnp.pad(jnp.where(here, rows, 0.0), ((0, 8 - rows.shape[0]), (0, 0)))
+
+
 def shards(
     residual, queries, keys, values, lengths, norm_gain, expert_ids, expert_weights, w_in, w_out
 ):
@@ -287,6 +747,15 @@
         "tgjl,tlgd->tgjd", attention_probs, value_rows, preferred_element_type=jnp.float32
     )
     summed = residual.astype(jnp.float32) + attended.reshape(tokens, width_local)
+    places = lax.axis_size("dp")
+    capacity = tokens * places * TOPK * 3 // (4 * EXPERTS)
+    planes = planes_of(places, tokens, width_local, w_in.shape[1], capacity)
+    if planes:
+        owners = places // EXPERTS
+        return layer(
+            summed, norm_gain[None, :], named_tile(expert_ids, expert_weights, planes * owners),
+            w_in, w_out, EXPERTS // planes, planes, owners, capacity, 3,
+        )
     square_sums = lax.psum(jnp.sum(summed * summed, axis=1), "tensor")
     normed = (
         summed
@@ -300,10 +769,8 @@
         (jnp.cumsum(onehot, axis=0, dtype=jnp.int32) - onehot) * onehot, axis=1, dtype=jnp.int32
     )
     counts = jnp.sum(onehot, axis=0, dtype=jnp.int32)
-    places = lax.axis_size("dp")
     me = lax.axis_index("dp")
     owners = places // EXPERTS
-    capacity = tokens * places * TOPK * 3 // (4 * EXPERTS)
     slot_total = EXPERTS * SRC_CAP
     pair_target = flat_ids * SRC_CAP + local_rank
     pick_pairs = pair_target[None, :] == jnp.arange(slot_total, dtype=jnp.int32)[:, None]

time: 114 us -> 86.1 us (0.76)
  matrix products: 37.7 us -> 8.16 us
  Pallas kernels: 66.9 us -> 71.8 us
  blocking collectives: 2.62 us -> 0 us
    dot_general x4 -> x0, matrix products: 29.5 us -> none  [the longest x1 14.1 us: shards(): jnp.einsum('cr,cd->rd', pick_rows, results, preferred_element_type=jnp.fl...]
    pallas_call x3 -> x1, Pallas kernels: 66.9 us -> 71.8 us  [layer(): pl.pallas_call(functools.partial(layer_kernel, (lines, planes, owners, ch...]
    psum x1 -> x0, blocking collectives: 2.62 us -> none  [shards(): square_sums = lax.psum(jnp.sum(summed * summed, axis=1), 'tensor')]
where the time goes in v1:
time: 86.1 us; the launch traced here: 85.8 us
  Pallas kernels  71.8 us (83%)
  matrix products  8.16 us (9%)
  local copies, waits for them, and re-layouts  4.22 us (5%)
  other arithmetic  1.53 us (2%)
    pallas_call x1, Pallas kernels, layer(): pl.pallas_call(functools.partial(layer_kernel, (lines, planes, owners, ch...  71.8 us
    sub x1, matrix products, shards(): powered = jnp.exp(scores - peak_score)  4.64 us
    dot_general x1, matrix products, shards(): jnp.einsum('tgjl,tlgd->tgjd', attention_probs, value_rows, preferred_elem...  3.52 us

profile of v1, /device:TPU:0, one launch (start us, length us, event | category | flops | bytes accessed | tf_op | source)
XLA Modules:
  0.0 85.8 jit_solution(7700108992214370336)
XLA Ops:
  0.0 1.2 %reshape.74 = bf16[32,4,6,128]{3,2,1,0:T(8,128)(2,1)S(1)} reshape(bf16[32,3072]{1,0:T(8,128)(2,1)} %param.11) | data formatting | bytes 393216 | tf_op jit(solution)/shard_map/reshape | solution.py:735
  1.2 0.7 iota_compare_fusion
  1.9 4.6 %fusion.17 = (f32[32,4,6]{2,1,0:T(4,128)S(1)}, f32[32,4,6,128]{3,2,1,0:T(8,128)S(1)}) fusion(bf16[32,4,6,128]{3,2,1,0:T(8,128)(2,1)S(1)} %reshape.74, pred[32,128]{1,0:T(8,128)(4,1)S(1)} %iota_compare_fusion, bf16[32,128,512]{2,1,0:T(8,128)(2,1)} %param.12), kind=kOutput, calls=%fused_computation.22 | convolution fusion | flops 25559168 | bytes 4791296 | tf_op jit(solution)/shard_map/sub | solution.py:744
  6.6 0.0 copy-start
  6.6 0.0 copy-start.1
  6.6 0.0 copy-start.2
  6.6 0.0 copy-start.3
  6.6 3.5 %fusion.1 = f32[32,4,6,128]{3,2,1,0:T(8,128)S(1)} fusion(f32[32,4,6,128]{3,2,1,0:T(8,128)S(1)} %get-tuple-element.6, f32[32,4,6]{2,1,0:T(4,128)S(1)} %get-tuple-element.5, bf16[32,128,512]{2,1,0:T(8,128)(2,1)} %param.13), kind=kOutput, calls=%fused_computation.1 | convolution fusion | flops 25362432 | bytes 4983808 | tf_op jit(solution)/shard_map/tgjl,tlgd->tgjd/dot_general | solution.py:746
  10.1 0.1 reshape.77
  10.2 0.0 copy-done
  10.3 0.8 convert_add_fusion.summed
  11.0 0.0 copy-done.1
  11.0 0.6 broadcast_in_dim.35.gain
  11.6 0.0 copy-done.2
  11.6 0.0 copy-done.3
  11.7 0.1 tile.10
  11.8 0.6 pad.4.named
  12.4 71.8 %shard_map.100 = bf16[32,3072]{1,0:T(8,128)(2,1)} custom-call(f32[32,3072]{1,0:T(8,128)} %convert_add_fusion.summed, bf16[1,3072]{1,0:T(2,128)(2,1)} %broadcast_in_dim.35.gain, f32[8,128]{1,0:T(8,128)} %pad.4.named, bf16[3072,4096]{1,0:T(8,128)(2,1)} %w_in.1, bf16[4096,3072]{1,0:T(8,128)(2,1)} %w_out.1), custom_call_target="tpu_custom_call" | custom-call | tf_op jit(solution)/shard_map/pallas_call | solution.py:660
  84.2 1.6 %copy.32 = bf16[32,3072]{1,0:T(8,128)(2,1)} copy(bf16[32,3072]{1,0:T(8,128)(2,1)} %shard_map.100) | data formatting | bytes 393216
  (5 shorter events, 0.0 us)
Async XLA Ops:
  6.6 3.7 %copy-start = (bf16[32,3072]{1,0:T(8,128)(2,1)S(1)}, bf16[32,3072]{1,0:T(8,128)(2,1)}, u32[]{:S(2)}) copy-start(bf16[32,3072]{1,0:T(8,128)(2,1)} %param.10) | copy-start | bytes 589828
  6.6 4.5 %copy-start.1 = (bf16[3072]{0:T(1024)(128)(2,1)S(1)}, bf16[3072]{0:T(1024)(128)(2,1)}, u32[]{:S(2)}) copy-start(bf16[3072]{0:T(1024)(128)(2,1)} %param.15) | copy-start | bytes 18436
  6.6 5.1 %copy-start.2 = (s32[32,2]{0,1:T(2,128)S(1)}, s32[32,2]{0,1:T(2,128)}, u32[]{:S(2)}) copy-start(s32[32,2]{0,1:T(2,128)} %param.16) | copy-start | bytes 772
  6.6 5.0 %copy-start.3 = (f32[32,2]{0,1:T(2,128)S(1)}, f32[32,2]{0,1:T(2,128)}, u32[]{:S(2)}) copy-start(f32[32,2]{0,1:T(2,128)} %param.17) | copy-start | bytes 772

commit v2 on v1

--- a/solution.py
+++ b/solution.py
@@ -269,13 +269,13 @@
     return -(-rows // 128) * 128
 
 
-def layer_kernel(dims, summed, gain, named, w_in, w_out, out, win, wout, squares, squares_in, gath,
-                 nrm, tok, pick, pick_t, slot_weight, sendx, gotx, acc, part, part_in, hidden,
+def layer_kernel(dims, residual, queries, keys, values, lengths, gain, names, shares, w_in, w_out,
+                 out, win, wout, summed, heads, named, squares, squares_in, gath, nrm, tok, pick, pick_t, slot_weight, sendx, gotx, acc, part, part_in, hidden,
                  sendy, goty, weighted, line_out, line_in, fin, extra,
-                 in_sem, out_sem, sq_sem, gath_sem, first_sem, line_sem, third_sem, part_sem,
+                 kv_sem, in_sem, out_sem, sq_sem, gath_sem, first_sem, line_sem, third_sem, part_sem,
                  back_sem, relay_sem, home_sem):
     lines, planes, owners, chunks, capacity = dims
-    tokens, width = summed.shape
+    tokens, width = residual.shape
     members = planes * owners
     places = lines * members
     quarter = width // members
@@ -289,11 +289,17 @@
     other_core = 1 - lax.axis_index("tensor")
     f32, bf16 = jnp.float32, jnp.bfloat16
 
-    def far(source, target, sems, index, device):
+    def far(source, target, send, recv, device):
         return pltpu.make_async_remote_copy(
-            src_ref=source, dst_ref=target, send_sem=sems.at[(0,) + index],
-            recv_sem=sems.at[(1,) + index], device_id=device, device_id_type=MESH,
+            src_ref=source, dst_ref=target, send_sem=send, recv_sem=recv, device_id=device,
+            device_id_type=MESH,
         )
+
+    def arrived(shape_like, recv):
+        far(shape_like, shape_like, recv, recv, {"tensor": other_core}).wait_recv()
+
+    def departed(shape_like, send):
+        far(shape_like, shape_like, send, send, {"tensor": other_core}).wait_send()
 
     def peer(step):
         return lax.rem(spot + step, members)
@@ -305,22 +311,38 @@
         return {"dp": line * members + index}
 
     steps = range(1, members)
-    win_copies = [
-        [
+    last = members - 1
+    depth = members * cols
+    width_kv = keys.shape[1]
+    cache = keys.shape[0] // tokens
+    per_kv = width_kv // HEAD
+    per_group = HEADS // KV
+    count = width // HEAD
+    batches = kv_sem.shape[0]
+    batch = tokens // batches
+
+    def kv_copies(i):
+        rows = pl.ds(i * batch * cache, batch * cache)
+        return [
+            pltpu.make_async_copy(keys.at[rows], wout.at[rows, pl.ds(0, width_kv)], kv_sem.at[i]),
             pltpu.make_async_copy(
-                w_in.at[pl.ds(q * quarter + c * cols, cols)],
-                win.at[pl.ds((c * members + q) * cols, cols)],
-                in_sem.at[c, q],
-            )
-            for q in range(members)
+                values.at[rows], wout.at[rows, pl.ds(width_kv, width_kv)], kv_sem.at[i]
+            ),
         ]
-        for c in range(chunks)
-    ]
-    pieces = out_sem.shape[0]
+
+    def win_copy(i):
+        c, q = lax.div(i, members), lax.rem(i, members)
+        return pltpu.make_async_copy(
+            w_in.at[pl.ds(pl.multiple_of(q * quarter + c * cols, cols), cols)],
+            win.at[pl.ds(pl.multiple_of(i * cols, cols), cols)],
+            in_sem.at[c],
+        )
+
+    pieces = 8
     piece = units // pieces
     wout_copies = [
         pltpu.make_async_copy(
-            w_out.at[pl.ds(i * piece, piece)], wout.at[pl.ds(i * piece, piece)], out_sem.at[i]
+            w_out.at[pl.ds(i * piece, piece)], wout.at[pl.ds(i * piece, piece)], out_sem.at[0]
         )
         for i in range(pieces)
     ]
@@ -330,25 +352,71 @@
             barrier, inc=1, device_id={"dp": lax.rem(me + lap, places)}, device_id_type=MESH
         )
     pl.semaphore_signal(barrier, inc=1, device_id={"tensor": other_core}, device_id_type=MESH)
-    for row in win_copies:
-        for copy in row:
+    for i in range(batches):
+        for copy in kv_copies(i):
             copy.start()
+    lane = lax.broadcasted_iota(jnp.int32, (8, group), 1)
+    here = (lane >= spot * tokens) & (lane < spot * tokens + tokens)
+    labels = jnp.concatenate([names[...].astype(f32), shares[...], jnp.zeros((4, tokens), f32)], axis=0)
+    named[...] = jnp.where(here, jnp.concatenate([labels] * members, axis=1), 0.0)
+    for h in range(count):
+        heads[pl.ds(h, tokens, stride=count)] = queries[:, h * HEAD:(h + 1) * HEAD].astype(f32)
+    head_row = lax.broadcasted_iota(jnp.int32, (count, HEAD), 0)
+    owned = [
+        (head_row >= g * per_group) & (head_row < (g + 1) * per_group) for g in range(per_kv)
+    ]
+    position = lax.broadcasted_iota(jnp.int32, (count, cache), 1)
+    feeds = -(-members * chunks // batches)
+
+    @pl.loop(0, batches)
+    def _(i):
+        rows = pl.ds(i * batch * cache, batch * cache)
+        whole = wout.at[rows, pl.ds(0, 2 * width_kv)]
+        pltpu.make_async_copy(w_out.at[pl.ds(0, batch * cache), pl.ds(0, 2 * width_kv)], whole,
+                              kv_sem.at[i]).wait()
+        for k in range(feeds):
+            @pl.when(i * feeds + k < members * chunks)
+            def _():
+                win_copy(i * feeds + k).start()
+        probs = []
+        for j in range(batch):
+            t = i * batch + j
+            query = heads[pl.ds(pl.multiple_of(t * count, 8), count)]
+            query = jnp.concatenate(
+                [jnp.where(mask, query, 0.0) for mask in owned], axis=1
+            ).astype(bf16)
+            key = wout[pl.ds(pl.multiple_of(t * cache, cache), cache), 0:width_kv]
+            score = lax.dot_general(query, key, (((1,), (1,)), ((), ())),
+                                    preferred_element_type=f32) * HEAD ** (-0.5)
+            score = jnp.where(position < lengths[t], score, -1e30)
+            powered = jnp.exp(score - jnp.max(score, axis=1, keepdims=True))
+            probs.append(
+                (powered / jnp.sum(powered, axis=1, keepdims=True)).astype(bf16)
+            )
+        for j in range(batch):
+            t = i * batch + j
+            value = wout[pl.ds(pl.multiple_of(t * cache, cache), cache), width_kv:2 * width_kv]
+            mixed = jnp.dot(probs[j], value, preferred_element_type=f32)
+            attended = jnp.where(owned[0], mixed[:, 0:HEAD], 0.0)
+            for g in range(1, per_kv):
+                attended += jnp.where(owned[g], mixed[:, g * HEAD:(g + 1) * HEAD], 0.0)
+            heads[pl.ds(pl.multiple_of(t * count, 8), count)] = attended
+
     for copy in wout_copies:
         copy.start()
     total = jnp.zeros((tokens, 1), f32)
-    for q in range(members * chunks):
-        value = summed[:, q * cols:(q + 1) * cols]
+    for h in range(count):
+        at = h * HEAD
+        value = residual[:, at:at + HEAD].astype(f32) + heads[pl.ds(h, tokens, stride=count)]
+        summed[:, at:at + HEAD] = value
         total += jnp.sum(value * value, axis=1, keepdims=True)
     squares[...] = jnp.broadcast_to(total, squares.shape)
     pl.semaphore_wait(barrier, places)
-    waiting = []
-    square_copy = far(squares, squares_in, sq_sem, (), {"tensor": other_core})
+    square_copy = far(squares, squares_in, sq_sem.at[0], sq_sem.at[1], {"tensor": other_core})
     square_copy.start()
-    waiting.append(square_copy)
     for lap in range(1, places):
-        copy = far(named, gath.at[me], gath_sem, (lap,), {"dp": lax.rem(me + lap, places)})
-        copy.start()
-        waiting.append(copy)
+        far(named, gath.at[me], gath_sem.at[0], gath_sem.at[1],
+            {"dp": lax.rem(me + lap, places)}).start()
     gath[me] = named[...]
     square_copy.wait_recv()
     scale = lax.rsqrt(
@@ -363,10 +431,8 @@
         home = pl.ds(pl.multiple_of(line * group + spot * tokens, tokens), tokens)
         tok[c, home] = nrm[spot, c]
         for step in steps:
-            copy = far(nrm.at[peer(step), c], tok.at[c, home], first_sem, (c, step),
-                       place(peer(step)))
-            copy.start()
-            waiting.append(copy)
+            far(nrm.at[peer(step), c], tok.at[c, home], first_sem.at[chunks], first_sem.at[c],
+                place(peer(step))).start()
 
     def rows_of(plane):
         return pl.ds(pl.multiple_of(plane * group, group), group)
@@ -379,43 +445,28 @@
         plane = line - gap * turn
         rows = rows_of(plane)
         return inside(plane) & inside(line + turn), far(
-            tok.at[c, rows], tok.at[c, rows], line_sem, (way, c, plane),
-            {"dp": me + turn * members},
+            tok.at[c, rows], tok.at[c, rows], line_sem.at[2 * chunks * lines + way],
+            line_sem.at[(way * chunks + c) * lines + plane], {"dp": me + turn * members},
         )
 
     def arrive(way, c, gap):
         plane = line - gap * (1 - 2 * way)
-        rows = rows_of(plane)
-        return inside(plane), far(
-            tok.at[c, rows], tok.at[c, rows], line_sem, (way, c, plane), {"dp": me}
-        )
+
+        @pl.when(inside(plane))
+        def _():
+            arrived(tok.at[c, rows_of(plane)], line_sem.at[(way * chunks + c) * lines + plane])
 
     def begin(pair):
         @pl.when(pair[0])
         def _():
             pair[1].start()
 
-    def landed(pair):
-        @pl.when(pair[0])
-        def _():
-            pair[1].wait_recv()
-
-    def left(pair):
-        @pl.when(pair[0])
-        def _():
-            pair[1].wait_send()
-
     for c in range(chunks):
-        for step in steps:
-            rows = pl.ds(pl.multiple_of(line * group + sender(step) * tokens, tokens), tokens)
-            far(nrm.at[0, c], tok.at[c, rows], first_sem, (c, step),
-                place(sender(step))).wait_recv()
+        arrived(nrm.at[pl.ds(0, last), c], first_sem.at[c])
         for way in (0, 1):
             begin(spread(way, c, 0))
 
-    for lap in range(1, places):
-        source = lax.rem(me + places - lap, places)
-        far(named, gath.at[source], gath_sem, (lap,), {"dp": source}).wait_recv()
+    arrived(gath.at[pl.ds(0, places - 1)], gath_sem.at[1])
     hits, weights = [], []
     for p in range(lines):
         tile = gath[p * members]
@@ -449,7 +500,6 @@
     def lanes_of(index):
         return pl.ds(pl.multiple_of(index * cols, 128), cols)
 
-    depth = members * cols
     block = 512
     spans = part.shape[0]
     span = units // spans
@@ -460,11 +510,9 @@
                        preferred_element_type=f32)
 
     def expand(c):
-        for step in steps:
-            far(sendx.at[c, 0], gotx.at[c, :, lanes_of(sender(step))], third_sem, (c, step),
-                place(sender(step))).wait_recv()
-        for copy in win_copies[c]:
-            copy.wait()
+        arrived(goty.at[c, pl.ds(0, last)], third_sem.at[c])
+        pltpu.make_async_copy(w_in.at[pl.ds(0, depth)], win.at[pl.ds(c * depth, depth)],
+                              in_sem.at[c]).wait()
         if c < chunks - 1:
             @pl.loop(0, units // block)
             def _(i):
@@ -481,29 +529,26 @@
                 if c:
                     value += acc[:, pl.ds(pl.multiple_of(at, block), block)]
                 part[h, :, pl.ds(inner, block)] = value.astype(bf16)
-            copy = far(part.at[h], part_in.at[h], part_sem, (h,), {"tensor": other_core})
-            copy.start()
-            waiting.append(copy)
+            far(part.at[h], part_in.at[h], part_sem.at[spans], part_sem.at[h],
+                {"tensor": other_core}).start()
 
     for c in range(chunks):
         for gap in range(1, lines):
             for way in (0, 1):
-                landed(arrive(way, c, gap))
+                arrive(way, c, gap)
                 begin(spread(way, c, gap))
         rows = jnp.dot(pick[...], tok[c], preferred_element_type=f32).astype(bf16)
         for b in range(planes):
             sendx[c, b] = rows[b * slots:b * slots + capacity]
         for step in steps:
-            copy = far(sendx.at[c, lax.div(peer(step), owners)], gotx.at[c, :, lanes_of(spot)],
-                       third_sem, (c, step), place(peer(step)))
-            copy.start()
-            waiting.append(copy)
+            far(sendx.at[c, lax.div(peer(step), owners)], gotx.at[c, :, lanes_of(spot)],
+                third_sem.at[chunks], third_sem.at[c], place(peer(step))).start()
         gotx[c, :, lanes_of(spot)] = sendx[c, own_plane]
         if c:
             expand(c - 1)
     expand(chunks - 1)
     for h in range(spans):
-        far(part.at[h], part_in.at[h], part_sem, (h,), {"tensor": other_core}).wait_recv()
+        arrived(part_in.at[h], part_sem.at[h])
 
         @pl.loop(0, span // block)
         def _(i):
@@ -513,8 +558,7 @@
             hidden[:, pl.ds(pl.multiple_of(h * span + i * block, block), block)] = (
                 value.astype(bf16)
             )
-    for copy in wout_copies:
-        copy.wait()
+    pltpu.make_async_copy(w_out, wout, out_sem.at[0]).wait()
 
     def contract(c):
         for step in list(steps) + [0]:
@@ -522,17 +566,13 @@
             value = jnp.dot(hidden[...], wout[:, pl.ds(at, cols)], preferred_element_type=f32)
             if step:
                 sendy[c, step - 1] = value.astype(bf16)
-                copy = far(sendy.at[c, step - 1], goty.at[c, spot], back_sem, (c, step),
-                           place(peer(step)))
-                copy.start()
-                waiting.append(copy)
+                far(sendy.at[c, step - 1], goty.at[c, spot], back_sem.at[chunks], back_sem.at[c],
+                    place(peer(step))).start()
             else:
                 goty[c, spot] = value.astype(bf16)
 
     def gather_back(c):
-        for step in steps:
-            far(sendy.at[c, 0], goty.at[c, sender(step)], back_sem, (c, step),
-                place(sender(step))).wait_recv()
+        arrived(sendy.at[c], back_sem.at[c])
         for b in range(planes):
             value = goty[c, b * owners].astype(f32)
             for o in range(1, owners):
@@ -543,9 +583,8 @@
     def share(c, plane):
         return jnp.dot(pick_t[plane], weighted[c], preferred_element_type=f32)
 
-    def relay_copy(way, c, plane, place_index):
-        return far(line_out.at[way, c, plane], line_in.at[way, c, plane], relay_sem,
-                   (way, c, plane), {"dp": place_index})
+    def relay_mark(way, c, plane):
+        return relay_sem.at[(way * chunks + c) * lines + plane]
 
     def relay(way, c, gap):
         turn = 1 - 2 * way
@@ -558,27 +597,24 @@
 
             @pl.when(inside(line - turn))
             def _():
-                relay_copy(way, c, plane, me - turn * members).wait_recv()
+                arrived(line_in.at[way, c, plane], relay_mark(way, c, plane))
                 line_out[way, c, plane] = (
                     value + line_in[way, c, plane].astype(f32)
                 ).astype(bf16)
 
-            relay_copy(way, c, plane, me + turn * members).start()
+            far(line_out.at[way, c, plane], line_in.at[way, c, plane],
+                relay_sem.at[2 * chunks * lines + way], relay_mark(way, c, plane),
+                {"dp": me + turn * members}).start()
 
     near = jnp.where(line * 2 < lines, 0, 1)
 
-    def home_copy(c, step):
-        rows = pl.ds(pl.multiple_of(peer(step) * tokens, tokens), tokens)
-        return far(fin.at[c, rows], extra.at[c, spot], home_sem, (c, step), place(peer(step)))
-
     def finish(c):
-        fin[c] = share(c, line).astype(bf16)
         for way in (0, 1):
             turn = 1 - 2 * way
 
             @pl.when(inside(line - turn))
             def _():
-                relay_copy(way, c, line, me - turn * members).wait_recv()
+                arrived(line_in.at[way, c, line], relay_mark(way, c, line))
 
         low, high = line > 0, line < lines - 1
 
@@ -598,15 +634,13 @@
             fin[c] = (share(c, line) + got(1)).astype(bf16)
 
         for step in steps:
-            copy = home_copy(c, step)
-            copy.start()
-            waiting.append(copy)
+            rows = pl.ds(pl.multiple_of(peer(step) * tokens, tokens), tokens)
+            far(fin.at[c, rows], extra.at[c, spot], home_sem.at[chunks], home_sem.at[c],
+                place(peer(step))).start()
         extra[c, spot] = fin[c, pl.ds(pl.multiple_of(spot * tokens, tokens), tokens)]
 
     def close(c):
-        for step in steps:
-            far(fin.at[c, pl.ds(0, tokens)], extra.at[c, sender(step)], home_sem, (c, step),
-                place(sender(step))).wait_recv()
+        arrived(extra.at[c, pl.ds(0, last)], home_sem.at[c])
         for q in range(members):
             at = q * quarter + c * cols
             out[:, at:at + cols] = (
@@ -632,27 +666,36 @@
         if c:
             close(c - 1)
     close(chunks - 1)
-    for copy in waiting:
-        copy.wait_send()
-    for c in range(chunks):
-        for way in (0, 1):
-            for gap in range(lines - 1):
-                left(spread(way, c, gap))
-            turn = 1 - 2 * way
-            for gap in range(1, lines):
-                plane = line + gap * turn
-                left((inside(plane), relay_copy(way, c, plane, me + turn * members)))
-
-
-def layer(summed, gain, named, w_in, w_out, lines, planes, owners, capacity, chunks):
-    tokens, width = summed.shape
+    departed(squares, sq_sem.at[0])
+    departed(gath.at[pl.ds(0, places - 1)], gath_sem.at[0])
+    departed(nrm.at[pl.ds(0, last)], first_sem.at[chunks])
+    departed(goty.at[:, pl.ds(0, last)], third_sem.at[chunks])
+    departed(part, part_sem.at[spans])
+    departed(sendy, back_sem.at[chunks])
+    departed(extra.at[:, pl.ds(0, last)], home_sem.at[chunks])
+    base = 2 * chunks * lines
+    for at in range(lines):
+        @pl.when(line == at)
+        def _():
+            above, below = lines - 1 - at, at
+            if above:
+                departed(tok.at[:, pl.ds(0, (below + 1) * group)], line_sem.at[base])
+                departed(line_out.at[0, :, pl.ds(0, above)], relay_sem.at[base])
+            if below:
+                departed(tok.at[:, pl.ds(0, (above + 1) * group)], line_sem.at[base + 1])
+                departed(line_out.at[1, :, pl.ds(0, below)], relay_sem.at[base + 1])
+
+
+def layer(residual, queries, keys, values, lengths, gain, names, shares, w_in, w_out, lines,
+          planes, owners, capacity, chunks):
+    tokens, width = residual.shape
     members = planes * owners
     cols = width // members // chunks
     places = lines * members
     group = members * tokens
     slots = slots_of(capacity)
     units = w_in.shape[1]
-    spans, pieces = 4, 8
+    spans, batches = 4, 4
     f32, bf16 = jnp.float32, jnp.bfloat16
     vmem = pl.BlockSpec(memory_space=pltpu.VMEM)
     hbm = pl.BlockSpec(memory_space=pl.ANY)
@@ -660,14 +703,18 @@
     return pl.pallas_call(
         functools.partial(layer_kernel, (lines, planes, owners, chunks, capacity)),
         out_shape=jax.ShapeDtypeStruct((tokens, width), bf16),
-        in_specs=[vmem, vmem, vmem, hbm, hbm],
+        in_specs=[vmem, vmem, hbm, hbm, pl.BlockSpec(memory_space=pltpu.SMEM), vmem, vmem, vmem,
+                  hbm, hbm],
         out_specs=vmem,
         scratch_shapes=[
             pltpu.VMEM(w_in.shape, bf16),
             pltpu.VMEM(w_out.shape, bf16),
+            pltpu.VMEM((tokens, width), f32),
+            pltpu.VMEM((tokens * width // HEAD, HEAD), f32),
+            pltpu.VMEM((8, group), f32),
             pltpu.VMEM((tokens, 128), f32),
             pltpu.VMEM((tokens, 128), f32),
-            pltpu.VMEM((places,) + named.shape, f32),
+            pltpu.VMEM((places, 8, group), f32),
             pltpu.VMEM((members, chunks, tokens, cols), bf16),
             pltpu.VMEM((chunks, lines * group, cols), bf16),
             pltpu.VMEM((planes * slots, lines * group), bf16),
@@ -686,25 +733,26 @@
             pltpu.VMEM((2, chunks, lines, group, cols), bf16),
             pltpu.VMEM((chunks, group, cols), bf16),
             pltpu.VMEM((chunks, members, tokens, cols), bf16),
-            dma((chunks, members)),
-            dma((pieces,)),
+            dma((batches,)),
+            dma((chunks,)),
+            dma((1,)),
             dma((2,)),
-            dma((2, places)),
-            dma((2, chunks, members)),
-            dma((2, 2, chunks, lines)),
-            dma((2, chunks, members)),
-            dma((2, spans)),
-            dma((2, chunks, members)),
-            dma((2, 2, chunks, lines)),
-            dma((2, chunks, members)),
+            dma((2,)),
+            dma((chunks + 1,)),
+            dma((2 * chunks * lines + 2,)),
+            dma((chunks + 1,)),
+            dma((spans + 1,)),
+            dma((chunks + 1,)),
+            dma((2 * chunks * lines + 2,)),
+            dma((chunks + 1,)),
         ],
         compiler_params=pltpu.CompilerParams(
             collective_id=3, has_side_effects=True, vmem_limit_bytes=63 * 1024 * 1024
         ),
-    )(summed, gain, named, w_in, w_out)
-
-
-def planes_of(places, tokens, width, units, capacity):
+    )(residual, queries, keys, values, lengths, gain, names, shares, w_in, w_out)
+
+
+def planes_of(places, tokens, width, width_kv, units, capacity):
     owners, rest = divmod(places, EXPERTS)
     planes = 2
     members = planes * owners
@@ -712,17 +760,10 @@
         return 0
     if width % (members * 128) or units % 2048 or capacity % 16:
         return 0
+    if tokens * CACHE > units or 2 * width_kv > width or CACHE % 128 or HEAD != 128:
+        return 0
     held = 4 * units * width + 12 * capacity * units
     return planes if held < 56 * 1024 * 1024 else 0
-
-
-def named_tile(expert_ids, expert_weights, members):
-    tokens = expert_ids.shape[0]
-    spot = lax.rem(lax.axis_index("dp"), members)
-    rows = jnp.concatenate([expert_ids.astype(jnp.float32), expert_weights], axis=1).T
-    rows = jnp.tile(rows, (1, members))
-    here = jnp.arange(members * tokens, dtype=jnp.int32)[None, :] // tokens == spot
-    return jnp.pad(jnp.where(here, rows, 0.0), ((0, 8 - rows.shape[0]), (0, 0)))
 
 
 def shards(
@@ -730,6 +771,16 @@
 ):
     tokens = residual.shape[0]
     width_local = residual.shape[1]
+    places = lax.axis_size("dp")
+    capacity = tokens * places * TOPK * 3 // (4 * EXPERTS)
+    width_kv = keys.shape[2]
+    planes = planes_of(places, tokens, width_local, width_kv, w_in.shape[1], capacity)
+    if planes:
+        return layer(
+            residual, queries, keys.reshape(-1, width_kv), values.reshape(-1, width_kv), lengths,
+            norm_gain[None, :], expert_ids.T, expert_weights.T, w_in, w_out, EXPERTS // planes,
+            planes, places // EXPERTS, capacity, 3,
+        )
     head_groups = keys.shape[2] // HEAD
     group_size = HEADS // KV
     query_rows = queries.reshape(tokens, head_groups, group_size, HEAD)
@@ -747,15 +798,6 @@
         "tgjl,tlgd->tgjd", attention_probs, value_rows, preferred_element_type=jnp.float32
     )
     summed = residual.astype(jnp.float32) + attended.reshape(tokens, width_local)
-    places = lax.axis_size("dp")
-    capacity = tokens * places * TOPK * 3 // (4 * EXPERTS)
-    planes = planes_of(places, tokens, width_local, w_in.shape[1], capacity)
-    if planes:
-        owners = places // EXPERTS
-        return layer(
-            summed, norm_gain[None, :], named_tile(expert_ids, expert_weights, planes * owners),
-            w_in, w_out, EXPERTS // planes, planes, owners, capacity, 3,
-        )
     square_sums = lax.psum(jnp.sum(summed * summed, axis=1), "tensor")
     normed = (
         summed

time: 86.1 us -> 74.5 us (0.87)
  matrix products: 8.16 us -> 0 us
  other arithmetic: 1.53 us -> 0 us
  local copies, waits for them, and re-layouts: 4.22 us -> 2.91 us
    sub x1 -> x0, matrix products: 4.64 us -> none  [shards(): powered = jnp.exp(scores - peak_score)]
    dot_general x1 -> x0, matrix products: 3.52 us -> none  [shards(): jnp.einsum('tgjl,tlgd->tgjd', attention_probs, value_rows, preferred_elem...]
    reshape x2 -> x0, local copies, waits for them, and re-layouts: 1.28 us -> none  [the longest x1 1.18 us: shards(): query_rows = queries.reshape(tokens, head_groups, group_size, HEAD)]
where the time goes in v2:
time: 74.5 us; the launch traced here: 74.3 us
  Pallas kernels  71.4 us (96%)
  local copies, waits for them, and re-layouts  2.91 us (4%)
    pallas_call x1, Pallas kernels, layer(): pl.pallas_call(functools.partial(layer_kernel, (lines, planes, owners, ch...  71.4 us
    unnamed x1, local copies, waits for them, and re-layouts  1.62 us

profile of v2, /device:TPU:0, one launch (start us, length us, event | category | flops | bytes accessed | tf_op | source)
XLA Modules:
  0.0 74.3 jit_solution(18090139360503983153)
XLA Ops:
  0.0 1.3 %broadcast_in_dim.3.gain = bf16[1,3072]{1,0:T(2,128)(2,1)} reshape(bf16[3072]{0:T(1024)(128)(2,1)} %param.15) | data formatting | bytes 12288 | tf_op jit(solution)/shard_map/broadcast_in_dim | solution.py:781
  1.3 71.4 %shard_map.100 = bf16[32,3072]{1,0:T(8,128)(2,1)} custom-call(bf16[32,3072]{1,0:T(8,128)(2,1)} %residual.1, bf16[32,3072]{1,0:T(8,128)(2,1)} %queries.1, bf16[4096,512]{1,0:T(8,128)(2,1)} %bitcast.4, bf16[4096,512]{1,0:T(8,128)(2,1)} %bitcast.5, s32[32]{0:T(128)} %lengths.1, bf16[1,3072]{1,0:T(2,128)(2,1)} %broadcast_in_dim.3.gain, s32[2,32]{1,0:T(2,128)} %bitcast.6, ...), custom_call_target="tpu_custom_call" | custom-call | tf_op jit(solution)/shard_map/pallas_call | solution.py:703
  72.7 1.6 %copy.12 = bf16[32,3072]{1,0:T(8,128)(2,1)} copy(bf16[32,3072]{1,0:T(8,128)(2,1)} %shard_map.100) | data formatting | bytes 393216

commit v3 on v2

--- a/solution.py
+++ b/solution.py
@@ -270,10 +270,10 @@
 
 
 def layer_kernel(dims, residual, queries, keys, values, lengths, gain, names, shares, w_in, w_out,
-                 out, win, wout, summed, heads, named, squares, squares_in, gath, nrm, tok, pick, pick_t, slot_weight, sendx, gotx, acc, part, part_in, hidden,
-                 sendy, goty, weighted, line_out, line_in, fin, extra,
-                 kv_sem, in_sem, out_sem, sq_sem, gath_sem, first_sem, line_sem, third_sem, part_sem,
-                 back_sem, relay_sem, home_sem):
+                 out, win, wout, summed, heads, named, slot_square, square_in, gath, tiles, nrm, tok, pick, pick_t, slot_weight, sendx, gotx, acc, part, part_in, hidden,
+                 sendy, goty, weighted, line_out, line_in, direct_in, fin, extra,
+                 kv_sem, in_sem, out_sem, sq_sem, gath_sem, tile_sem, first_sem, line_sem, third_sem, part_sem,
+                 back_sem, relay_sem, direct_sem, home_sem):
     lines, planes, owners, chunks, capacity = dims
     tokens, width = residual.shape
     members = planes * owners
@@ -310,6 +310,9 @@
     def place(index):
         return {"dp": line * members + index}
 
+    def along(gap):
+        return {"dp": lax.rem(line + gap, lines) * members + spot}
+
     steps = range(1, members)
     last = members - 1
     depth = members * cols
@@ -347,18 +350,14 @@
         for i in range(pieces)
     ]
     barrier = pltpu.get_barrier_semaphore()
-    for lap in range(1, places):
-        pl.semaphore_signal(
-            barrier, inc=1, device_id={"dp": lax.rem(me + lap, places)}, device_id_type=MESH
-        )
+    for step in steps:
+        pl.semaphore_signal(barrier, inc=1, device_id=place(peer(step)), device_id_type=MESH)
+    for gap in range(1, lines):
+        pl.semaphore_signal(barrier, inc=1, device_id=along(gap), device_id_type=MESH)
     pl.semaphore_signal(barrier, inc=1, device_id={"tensor": other_core}, device_id_type=MESH)
     for i in range(batches):
         for copy in kv_copies(i):
             copy.start()
-    lane = lax.broadcasted_iota(jnp.int32, (8, group), 1)
-    here = (lane >= spot * tokens) & (lane < spot * tokens + tokens)
-    labels = jnp.concatenate([names[...].astype(f32), shares[...], jnp.zeros((4, tokens), f32)], axis=0)
-    named[...] = jnp.where(here, jnp.concatenate([labels] * members, axis=1), 0.0)
     for h in range(count):
         heads[pl.ds(h, tokens, stride=count)] = queries[:, h * HEAD:(h + 1) * HEAD].astype(f32)
     head_row = lax.broadcasted_iota(jnp.int32, (count, HEAD), 0)
@@ -410,29 +409,36 @@
         value = residual[:, at:at + HEAD].astype(f32) + heads[pl.ds(h, tokens, stride=count)]
         summed[:, at:at + HEAD] = value
         total += jnp.sum(value * value, axis=1, keepdims=True)
-    squares[...] = jnp.broadcast_to(total, squares.shape)
-    pl.semaphore_wait(barrier, places)
-    square_copy = far(squares, squares_in, sq_sem.at[0], sq_sem.at[1], {"tensor": other_core})
-    square_copy.start()
-    for lap in range(1, places):
-        far(named, gath.at[me], gath_sem.at[0], gath_sem.at[1],
-            {"dp": lax.rem(me + lap, places)}).start()
-    gath[me] = named[...]
-    square_copy.wait_recv()
-    scale = lax.rsqrt(
-        (squares[:, :1] + squares_in[:, :1]) / (2 * width) + NORM_EPSILON
-    )
+    square_row = jnp.broadcast_to(total, (tokens, 128)).T[0:1]
+    lane = lax.broadcasted_iota(jnp.int32, (8, group), 1)
+    here = (lane >= spot * tokens) & (lane < spot * tokens + tokens)
+    labels = jnp.concatenate(
+        [names[...].astype(f32), shares[...], square_row, jnp.zeros((3, tokens), f32)], axis=0
+    )
+    named[...] = jnp.where(here, jnp.concatenate([labels] * members, axis=1), 0.0)
+    pl.semaphore_wait(barrier, members + lines - 1)
+    for step in steps:
+        far(named, gath.at[spot], gath_sem.at[0], gath_sem.at[1], place(peer(step))).start()
+    gath[spot] = named[...]
     for c in range(chunks):
         for q in range(members):
             at = q * quarter + c * cols
             nrm[q, c] = (
-                summed[:, at:at + cols] * scale * gain[:, at:at + cols].astype(f32)
+                summed[:, at:at + cols] * gain[at:at + cols].astype(f32)[None, :]
             ).astype(bf16)
         home = pl.ds(pl.multiple_of(line * group + spot * tokens, tokens), tokens)
         tok[c, home] = nrm[spot, c]
         for step in steps:
             far(nrm.at[peer(step), c], tok.at[c, home], first_sem.at[chunks], first_sem.at[c],
                 place(peer(step))).start()
+
+    arrived(gath.at[pl.ds(0, last)], gath_sem.at[1])
+    tile = gath[0]
+    for m in range(1, members):
+        tile += gath[m]
+    tiles[line] = tile
+    for gap in range(1, lines):
+        far(tiles.at[line], tiles.at[line], tile_sem.at[0], tile_sem.at[1], along(gap)).start()
 
     def rows_of(plane):
         return pl.ds(pl.multiple_of(plane * group, group), group)
@@ -466,12 +472,11 @@
         for way in (0, 1):
             begin(spread(way, c, 0))
 
-    arrived(gath.at[pl.ds(0, places - 1)], gath_sem.at[1])
-    hits, weights = [], []
+    arrived(tiles.at[pl.ds(0, lines - 1)], tile_sem.at[1])
+    hits, weights, tile_squares = [], [], []
     for p in range(lines):
-        tile = gath[p * members]
-        for m in range(1, members):
-            tile += gath[p * members + m]
+        tile = tiles[p]
+        tile_squares.append(tile[4:5])
         for b in range(planes):
             expert = (line * planes + b).astype(f32)
             first, second = tile[0:1] == expert, tile[1:2] == expert
@@ -484,6 +489,7 @@
     for b in range(planes):
         offset = jnp.zeros((1, 1), f32)
         slot_total = jnp.zeros((slots, 1), f32)
+        square_total = jnp.zeros((slots, 1), f32)
         for p in range(lines):
             hit, weight = hits[p * planes + b], weights[p * planes + b]
             wide = jnp.broadcast_to(hit, (16, group)).astype(bf16)
@@ -494,43 +500,43 @@
             pick[b * slots:(b + 1) * slots, p * group:(p + 1) * group] = chosen.astype(bf16)
             pick_t[p, :, b * slots:(b + 1) * slots] = chosen.T.astype(bf16)
             slot_total += jnp.sum(chosen * weight, axis=1, keepdims=True)
+            square_total += jnp.sum(chosen * tile_squares[p], axis=1, keepdims=True)
         slot_weight[b * slots:(b + 1) * slots] = jnp.broadcast_to(slot_total, (slots, 128))
+        slot_square[b * slots:(b + 1) * slots] = jnp.broadcast_to(square_total, (slots, 128))
+    own_slots = pl.multiple_of(own_plane * slots, slots)
+    far(slot_square.at[pl.ds(own_slots, slots)], square_in, sq_sem.at[0], sq_sem.at[1],
+        {"tensor": other_core}).start()
     weighted[...] = jnp.zeros_like(weighted)
 
     def lanes_of(index):
         return pl.ds(pl.multiple_of(index * cols, 128), cols)
 
-    block = 512
     spans = part.shape[0]
     span = units // spans
+    block = 512
+    slab = 256
 
     def product(c, at):
-        at = pl.multiple_of(at, 128)
-        return jnp.dot(gotx[c], win[c * depth:(c + 1) * depth, pl.ds(at, block)],
-                       preferred_element_type=f32)
+        return jnp.dot(gotx[c], win[c * depth:(c + 1) * depth, at], preferred_element_type=f32)
 
     def expand(c):
         arrived(goty.at[c, pl.ds(0, last)], third_sem.at[c])
         pltpu.make_async_copy(w_in.at[pl.ds(0, depth)], win.at[pl.ds(c * depth, depth)],
                               in_sem.at[c]).wait()
-        if c < chunks - 1:
-            @pl.loop(0, units // block)
-            def _(i):
-                at = pl.multiple_of(i * block, block)
-                value = product(c, at)
-                acc[:, pl.ds(at, block)] = value if c == 0 else acc[:, pl.ds(at, block)] + value
-            return
-        for h in range(spans):
-            @pl.loop(0, span // block)
-            def _(i):
-                inner = pl.multiple_of(i * block, block)
-                at = h * span + inner
+        @pl.loop(0, spans)
+        def _(h):
+            for inner in range(0, span, slab):
+                at = pl.ds(pl.multiple_of(h * span + inner, slab), slab)
                 value = product(c, at)
                 if c:
-                    value += acc[:, pl.ds(pl.multiple_of(at, block), block)]
-                part[h, :, pl.ds(inner, block)] = value.astype(bf16)
-            far(part.at[h], part_in.at[h], part_sem.at[spans], part_sem.at[h],
-                {"tensor": other_core}).start()
+                    value += acc[:, at]
+                if c < chunks - 1:
+                    acc[:, at] = value
+                else:
+                    part[h, :, inner:inner + slab] = value.astype(bf16)
+            if c == chunks - 1:
+                far(part.at[h], part_in.at[h], part_sem.at[spans], part_sem.at[h],
+                    {"tensor": other_core}).start()
 
     for c in range(chunks):
         for gap in range(1, lines):
@@ -547,29 +553,39 @@
         if c:
             expand(c - 1)
     expand(chunks - 1)
+    arrived(square_in, sq_sem.at[1])
+    scale = lax.rsqrt(
+        (slot_square[pl.ds(own_slots, capacity), :1] + square_in[0:capacity, :1]) / (2 * width)
+        + NORM_EPSILON
+    )
     for h in range(spans):
         arrived(part_in.at[h], part_sem.at[h])
 
         @pl.loop(0, span // block)
         def _(i):
             at = pl.ds(pl.multiple_of(i * block, block), block)
-            value = part[h, :, at].astype(f32) + part_in[h, :, at].astype(f32)
+            value = (part[h, :, at].astype(f32) + part_in[h, :, at].astype(f32)) * scale
             value = value / (1.0 + jnp.exp(-value))
             hidden[:, pl.ds(pl.multiple_of(h * span + i * block, block), block)] = (
                 value.astype(bf16)
             )
     pltpu.make_async_copy(w_out, wout, out_sem.at[0]).wait()
 
+    joined = 1
+
     def contract(c):
         for step in list(steps) + [0]:
             at = pl.multiple_of(peer(step) * quarter + c * cols, 128)
-            value = jnp.dot(hidden[...], wout[:, pl.ds(at, cols)], preferred_element_type=f32)
-            if step:
-                sendy[c, step - 1] = value.astype(bf16)
-                far(sendy.at[c, step - 1], goty.at[c, spot], back_sem.at[chunks], back_sem.at[c],
-                    place(peer(step))).start()
-            else:
-                goty[c, spot] = value.astype(bf16)
+            value = jnp.dot(hidden[...], wout[:, pl.ds(at, joined * cols)],
+                            preferred_element_type=f32).astype(bf16)
+            for k in range(joined):
+                inner = value[:, k * cols:(k + 1) * cols]
+                if step:
+                    sendy[c + k, step - 1] = inner
+                    far(sendy.at[c + k, step - 1], goty.at[c + k, spot], back_sem.at[chunks],
+                        back_sem.at[c + k], place(peer(step))).start()
+                else:
+                    goty[c + k, spot] = inner
 
     def gather_back(c):
         arrived(sendy.at[c], back_sem.at[c])
@@ -595,12 +611,17 @@
             value = share(c, plane)
             line_out[way, c, plane] = value.astype(bf16)
 
-            @pl.when(inside(line - turn))
-            def _():
-                arrived(line_in.at[way, c, plane], relay_mark(way, c, plane))
-                line_out[way, c, plane] = (
-                    value + line_in[way, c, plane].astype(f32)
-                ).astype(bf16)
+            if gap == lines - 1:
+                far(line_out.at[way, c, plane], direct_in.at[c], direct_sem.at[chunks],
+                    direct_sem.at[c], {"dp": me + turn * gap * members}).start()
+                return
+            if gap + 1 < lines - 1:
+                @pl.when(inside(line - turn))
+                def _():
+                    arrived(line_in.at[way, c, plane], relay_mark(way, c, plane))
+                    line_out[way, c, plane] = (
+                        value + line_in[way, c, plane].astype(f32)
+                    ).astype(bf16)
 
             far(line_out.at[way, c, plane], line_in.at[way, c, plane],
                 relay_sem.at[2 * chunks * lines + way], relay_mark(way, c, plane),
@@ -627,11 +648,13 @@
 
         @pl.when(low & ~high)
         def _():
-            fin[c] = (share(c, line) + got(0)).astype(bf16)
+            arrived(direct_in.at[c], direct_sem.at[c])
+            fin[c] = (share(c, line) + got(0) + direct_in[c].astype(f32)).astype(bf16)
 
         @pl.when(high & ~low)
         def _():
-            fin[c] = (share(c, line) + got(1)).astype(bf16)
+            arrived(direct_in.at[c], direct_sem.at[c])
+            fin[c] = (share(c, line) + got(1) + direct_in[c].astype(f32)).astype(bf16)
 
         for step in steps:
             rows = pl.ds(pl.multiple_of(peer(step) * tokens, tokens), tokens)
@@ -647,27 +670,25 @@
                 summed[:, at:at + cols] + extra[c, q].astype(f32)
             ).astype(out.dtype)
 
+    for c in range(0, chunks, joined):
+        contract(c)
     for c in range(chunks):
-        contract(c)
-        if c:
-            gather_back(c - 1)
-            for gap in range(lines - 1, 1, -1):
-                relay(near, c - 1, gap)
-    gather_back(chunks - 1)
-    for gap in range(lines - 1, 1, -1):
-        relay(near, chunks - 1, gap)
+        gather_back(c)
+        for gap in list(range(lines - 2, 1, -1)) + [lines - 1]:
+            relay(near, c, gap)
     for c in range(chunks):
         relay(near, c, 1)
     for c in range(chunks):
-        for gap in range(lines - 1, 0, -1):
+        for gap in range(lines - 2, 0, -1):
             relay(1 - near, c, gap)
     for c in range(chunks):
         finish(c)
         if c:
             close(c - 1)
     close(chunks - 1)
-    departed(squares, sq_sem.at[0])
-    departed(gath.at[pl.ds(0, places - 1)], gath_sem.at[0])
+    departed(square_in, sq_sem.at[0])
+    departed(gath.at[pl.ds(0, last)], gath_sem.at[0])
+    departed(tiles.at[pl.ds(0, lines - 1)], tile_sem.at[0])
     departed(nrm.at[pl.ds(0, last)], first_sem.at[chunks])
     departed(goty.at[:, pl.ds(0, last)], third_sem.at[chunks])
     departed(part, part_sem.at[spans])
@@ -680,10 +701,14 @@
             above, below = lines - 1 - at, at
             if above:
                 departed(tok.at[:, pl.ds(0, (below + 1) * group)], line_sem.at[base])
-                departed(line_out.at[0, :, pl.ds(0, above)], relay_sem.at[base])
+                sent = above if below else above - 1
+                departed(line_out.at[0, :, pl.ds(0, sent)], relay_sem.at[base])
             if below:
                 departed(tok.at[:, pl.ds(0, (above + 1) * group)], line_sem.at[base + 1])
-                departed(line_out.at[1, :, pl.ds(0, below)], relay_sem.at[base + 1])
+                sent = below if above else below - 1
+                departed(line_out.at[1, :, pl.ds(0, sent)], relay_sem.at[base + 1])
+            if not above or not below:
+                departed(direct_in, direct_sem.at[chunks])
 
 
 def layer(residual, queries, keys, values, lengths, gain, names, shares, w_in, w_out, lines,
@@ -712,9 +737,10 @@
             pltpu.VMEM((tokens, width), f32),
             pltpu.VMEM((tokens * width // HEAD, HEAD), f32),
             pltpu.VMEM((8, group), f32),
-            pltpu.VMEM((tokens, 128), f32),
-            pltpu.VMEM((tokens, 128), f32),
-            pltpu.VMEM((places, 8, group), f32),
+            pltpu.VMEM((planes * slots, 128), f32),
+            pltpu.VMEM((slots, 128), f32),
+            pltpu.VMEM((members, 8, group), f32),
+            pltpu.VMEM((lines, 8, group), f32),
             pltpu.VMEM((members, chunks, tokens, cols), bf16),
             pltpu.VMEM((chunks, lines * group, cols), bf16),
             pltpu.VMEM((planes * slots, lines * group), bf16),
@@ -732,10 +758,12 @@
             pltpu.VMEM((2, chunks, lines, group, cols), bf16),
             pltpu.VMEM((2, chunks, lines, group, cols), bf16),
             pltpu.VMEM((chunks, group, cols), bf16),
+            pltpu.VMEM((chunks, group, cols), bf16),
             pltpu.VMEM((chunks, members, tokens, cols), bf16),
             dma((batches,)),
             dma((chunks,)),
             dma((1,)),
+            dma((2,)),
             dma((2,)),
             dma((2,)),
             dma((chunks + 1,)),
@@ -745,6 +773,7 @@
             dma((chunks + 1,)),
             dma((2 * chunks * lines + 2,)),
             dma((chunks + 1,)),
+            dma((chunks + 1,)),
         ],
         compiler_params=pltpu.CompilerParams(
             collective_id=3, has_side_effects=True, vmem_limit_bytes=63 * 1024 * 1024
@@ -758,7 +787,7 @@
     members = planes * owners
     if rest or lax.axis_size("tensor") != 2 or members < 2 or members * tokens != 128:
         return 0
-    if width % (members * 128) or units % 2048 or capacity % 16:
+    if EXPERTS // planes < 3 or width % (members * 128) or units % 2048 or capacity % 16:
         return 0
     if tokens * CACHE > units or 2 * width_kv > width or CACHE % 128 or HEAD != 128:
         return 0
@@ -778,8 +807,8 @@
     if planes:
         return layer(
             residual, queries, keys.reshape(-1, width_kv), values.reshape(-1, width_kv), lengths,
-            norm_gain[None, :], expert_ids.T, expert_weights.T, w_in, w_out, EXPERTS // planes,
-            planes, places // EXPERTS, capacity, 3,
+            norm_gain, expert_ids.T, expert_weights.T, w_in, w_out, EXPERTS // planes,
+            planes, places // EXPERTS, capacity, 2,
         )
     head_groups = keys.shape[2] // HEAD
     group_size = HEADS // KV

time: 74.5 us -> 67.3 us (0.903)
  Pallas kernels: 71.4 us -> 65.5 us
  local copies, waits for them, and re-layouts: 2.91 us -> 1.62 us
    pallas_call x1, Pallas kernels: 71.4 us -> 65.5 us  [layer(): pl.pallas_call(functools.partial(layer_kernel, (lines, planes, owners, ch...]
    broadcast_in_dim x1 -> x0, local copies, waits for them, and re-layouts: 1.3 us -> none  [shards(): norm_gain[None, :]]
where the time goes in v3:
time: 67.3 us; the launch traced here: 67.2 us
  Pallas kernels  65.5 us (97%)
  local copies, waits for them, and re-layouts  1.62 us (2%)
    pallas_call x1, Pallas kernels, layer(): pl.pallas_call(functools.partial(layer_kernel, (lines, planes, owners, ch...  65.5 us
    unnamed x1, local copies, waits for them, and re-layouts  1.62 us

profile of v3, /device:TPU:0, one launch (start us, length us, event | category | flops | bytes accessed | tf_op | source)
XLA Modules:
  0.0 67.2 jit_solution(7223969074484161473)
XLA Ops:
  0.0 65.5 %shard_map.100 = bf16[32,3072]{1,0:T(8,128)(2,1)} custom-call(bf16[32,3072]{1,0:T(8,128)(2,1)} %residual.1, bf16[32,3072]{1,0:T(8,128)(2,1)} %queries.1, bf16[4096,512]{1,0:T(8,128)(2,1)} %bitcast.4, bf16[4096,512]{1,0:T(8,128)(2,1)} %bitcast.5, s32[32]{0:T(128)} %lengths.1, bf16[3072]{0:T(1024)(128)(2,1)} %gain.1, s32[2,32]{1,0:T(2,128)} %bitcast.6, ...), custom_call_target="tpu_custom_call" | custom-call | tf_op jit(solution)/shard_map/pallas_call | solution.py:728
  65.6 1.6 %copy.12 = bf16[32,3072]{1,0:T(8,128)(2,1)} copy(bf16[32,3072]{1,0:T(8,128)(2,1)} %shard_map.100) | data formatting | bytes 393216
